TPU v7x, 32 devices: a whole 2x2x4 slice. The times are simulated.
32 devices in a mesh: orient: 8 (over z, y), dom: 4 (over x, core).
Axes of the slice: x: 2, y: 2, z: 4, core: 2. Of those that a mesh axis runs over, the one named last changes fastest.
Arguments:
- particles: bfloat16 [256, 8448], P(('dom', 'orient')), parts along dimension 0, may hold values from -12 to 12
- defocus: float32 [256], P(('dom', 'orient')), parts along dimension 0, may hold values from 10 to 60
- inv_noise: float32 [4224], replicated, may hold values from 0.5 to 2
- references: bfloat16 [13824, 8448], P(('dom', 'orient')), parts along dimension 0, may hold values from -0.25 to 0.25
- thresholds: int32 [256], P('dom'), parts along dimension 0, may hold values from 512 to 1023
- range_start: int32 [256], P('dom'), parts along dimension 0, may hold values from 0 to 3455
- range_len: int32 [256], P('dom'), parts along dimension 0, may hold values from 36 to 1727
Outputs:
- posterior: float32 [256, 3456], P('dom', 'orient'), parts along dimension 0
- cumulative: float32 [256, 3456], P('dom', 'orient'), parts along dimension 0
- log_evidence: float32 [256], P('dom'), parts along dimension 0
- kept_mass: float32 [256], P('dom'), parts along dimension 0
There are 4 independent parts, one for each index of `dom`. A program takes and returns all parts, laid end to end along the dimension named above; an argument that names none is the same for every part. Nothing has to cross between parts.
All inputs are finite; a program needn't handle non-finite values.
Results may differ from a plain program's by a relative error of at most 0.0004.
The roundings to bfloat16 on the way count: a program that leaves them out, or rounds other values in their place, can miss the bound.
Values may be sent and summed in bfloat16 or wider, within the bound.
No kernel may reach another device: no remote copies, remote signals or barrier semaphores. Data moves between devices by JAX's collectives and lax.ppermute only.
A program may use at most 64 MiB of HBM per device.

v0:
```python
import math

import jax
import jax.numpy as jnp
from jax import lax
from jax.experimental import pallas as pl
from jax.experimental.pallas import tpu as pltpu
from jax.sharding import PartitionSpec as P


LANES = 128
VMEM = pl.BlockSpec(memory_space=pltpu.VMEM)
HBM = pl.BlockSpec(memory_space=pltpu.HBM)


def minus_sine(x):
    turns = jnp.floor(x * (1.0 / math.pi) + 0.5)
    rest = x - turns * 3.1414794921875
    rest = rest - turns * 0.00011315941810607910156
    rest = rest - turns * 1.9841872589410058936e-09
    sq = rest * rest
    poly = sq * 2.6083159809786593541503e-06 - 0.0001981069071916863322258
    poly = poly * sq + 0.00833307858556509017944336
    poly = poly * sq - 0.166666597127914428710938
    value = rest + rest * (sq * poly)
    half = turns * 0.5
    return value * ((half - jnp.floor(half)) * 4.0 - 1.0)


def column(row):
    size = row.shape[1]
    down = lax.broadcasted_iota(jnp.int32, (size, size), 0)
    across = lax.broadcasted_iota(jnp.int32, (size, size), 1)
    return jnp.sum(jnp.where(down == across, row, 0.0), axis=1, keepdims=True)


def pack_body(particles, defocus, out, row, sems):
    feat = particles.shape[1]
    copy = pltpu.make_async_copy(particles, out.at[:, pl.ds(0, feat)], sems.at[0])
    fetch = pltpu.make_async_copy(defocus, row, sems.at[1])
    fetch.start()
    copy.start()
    fetch.wait()
    value = column(row[...])
    high = value.astype(jnp.bfloat16).astype(jnp.float32)
    mid = (value - high).astype(jnp.bfloat16).astype(jnp.float32)
    low = value - high - mid
    lane = lax.broadcasted_iota(jnp.int32, (value.shape[0], LANES), 1)
    parts = jnp.where(lane == 0, high, jnp.where(lane == 1, mid, jnp.where(lane == 2, low, 0.0)))
    out[:, pl.ds(feat, LANES)] = parts.astype(jnp.bfloat16)
    copy.wait()


def focus_of(piece, cut):
    bits = piece[:, pl.ds(2 * cut, LANES)].astype(jnp.float32)
    value = bits[:, 0:1] + bits[:, 1:2] + bits[:, 2:3]
    return jnp.broadcast_to(value, (value.shape[0], LANES))


def frequencies(k):
    col_pos = (lax.broadcasted_iota(jnp.int32, (1, LANES), 1) - 64).astype(jnp.float32)
    row_pos = jnp.asarray(k // 128).astype(jnp.float32)
    return math.pi * (row_pos * row_pos + col_pos * col_pos) / 16384.0


def weigh(real, imag, focus, noise_row, freq):
    ctf = minus_sine(focus * freq + 0.07)
    power = (ctf * ctf * noise_row).astype(jnp.bfloat16).astype(jnp.float32)
    return real.astype(jnp.float32) * ctf * noise_row, imag.astype(jnp.float32) * ctf * noise_row, -0.5 * power


def product(left, left_at, right):
    dims = (((1,), (1,)), ((), ()))
    return lax.dot_general(left[:, left_at], right, dims, preferred_element_type=jnp.float32)


def contract(total, references, power, stage, first, last, base):
    coef = power.shape[1]
    span = stage.shape[1] // 3
    for left, shift, block in ((references, 0, 0), (references, coef, 1), (power, 0, 2)):
        right = stage[:, pl.ds(block * span + first - base, last - first)]
        part = product(left, pl.ds(shift + first, last - first), right)
        total = part if total is None else total + part
    return total


def fill(stage, row, base, pieces, focuses, noise, k):
    span = stage.shape[1] // 3
    rows = pieces[0][0].shape[0]
    for i in range(0, len(pieces), 2):
        values = [
            weigh(piece[:, pl.ds(real, LANES)], piece[:, pl.ds(imag, LANES)], focus, noise[pl.ds(k, LANES)].reshape(1, LANES), frequencies(k))
            for (piece, real, imag), focus in zip(pieces[i : i + 2], focuses[i : i + 2])
        ]
        for block, pair in enumerate(zip(*values)):
            at = pl.ds(block * span + k - base, LANES)
            stage[pl.ds(row + i * rows, len(pair) * rows), at] = jnp.concatenate(pair, axis=0).astype(jnp.bfloat16)


def weigh_body(noise, *refs):
    pieces, stage = refs[:-1], refs[-1]
    coef = stage.shape[1] // 3
    focuses = [focus_of(piece, coef) for piece in pieces]
    for k in range(0, coef, LANES):
        fill(stage, 0, 0, [(piece, k, coef + k) for piece in pieces], focuses, noise, k)


def score_late_body(*refs, row, all_orients):
    start, length, noise, references, power = refs[:5]
    pieces = refs[6:-3]
    scores, stats, stage = refs[-3:]
    coef = power.shape[1]
    focuses = [focus_of(piece, coef) for piece in pieces]
    total = None
    for first in range(0, coef, 2 * LANES):
        last = min(first + 2 * LANES, coef)
        for k in range(first, last, LANES):
            fill(stage, row, 0, [(piece, k, coef + k) for piece in pieces], focuses, noise, k)
        total = contract(total, references, power, stage, first, last, 0)
    scores[...] = total
    statistics(total, start, length, stats, all_orients, pieces[0].shape[0])


def reorder(x, rows, me):
    count = x.shape[1]
    x = jnp.concatenate([x] * (LANES // count), axis=1)
    lane = lax.broadcasted_iota(jnp.int32, x.shape, 1)
    step = rows
    while step < count:
        swapped = jnp.where((lane & step) != 0, pltpu.roll(x, step, 1), pltpu.roll(x, LANES - step, 1))
        x = jnp.where((me & (step // rows)) != 0, swapped, x)
        step *= 2
    return x[:, :count]


def statistics(total, start, length, stats, all_orients, rows=None):
    me = lax.axis_index("orient")
    base = me * total.shape[0]
    begin = start[...]
    end = begin + length[...]
    end = jnp.where(end > all_orients, end - all_orients, end) - base
    begin = begin - base
    if rows:
        begin = reorder(begin, rows, me)
        end = reorder(end, rows, me)
    top = jnp.max(total, axis=0, keepdims=True)
    expon = jnp.exp(total - top)
    index = lax.broadcasted_iota(jnp.int32, total.shape, 0)
    table = jnp.concatenate(
        [
            top,
            jnp.sum(expon, axis=0, keepdims=True),
            jnp.sum(jnp.where(index < begin, expon, 0.0), axis=0, keepdims=True),
            jnp.sum(jnp.where(index < end, expon, 0.0), axis=0, keepdims=True),
        ],
        axis=0,
    )
    stats[...] = reorder(table, rows, me) if rows else table


def power_body(references, local, out, sems):
    rows, coef = out.shape
    step = -(-rows // (8 * sems.shape[0])) * 8
    spans = [pl.ds(r, min(step, rows - r)) for r in range(0, rows, step)]
    copies = [pltpu.make_async_copy(references.at[span], local.at[span], sems.at[i]) for i, span in enumerate(spans)]
    for copy in copies:
        copy.start()
    for span, copy in zip(spans, copies):
        copy.wait()
        for k in range(0, coef, LANES):
            real = local[span, pl.ds(k, LANES)].astype(jnp.float32)
            imag = local[span, pl.ds(coef + k, LANES)].astype(jnp.float32)
            out[span, pl.ds(k, LANES)] = (real * real + imag * imag).astype(jnp.bfloat16)


def score_body(start, length, noise, references, power, packed, scores, stats, stage, *, all_orients):
    coef = power.shape[1]
    step = 2 * LANES
    scores[...] = jnp.zeros(scores.shape, jnp.float32)

    def chunk(first, width):
        focus = focus_of(packed, coef)
        for k in range(0, width, LANES):
            noise_row = noise[pl.ds(first + k, LANES)].reshape(1, LANES)
            real = packed[:, pl.ds(first + k, LANES)]
            imag = packed[:, pl.ds(coef + first + k, LANES)]
            values = weigh(real, imag, focus, noise_row, frequencies(first + k))
            for block, value in enumerate(values):
                stage[:, pl.ds(block * step + k, LANES)] = value.astype(jnp.bfloat16)
        total = product(references, pl.ds(first, width), stage[:, pl.ds(0, width)])
        total = total + product(references, pl.ds(coef + first, width), stage[:, pl.ds(step, width)])
        scores[...] += total + product(power, pl.ds(first, width), stage[:, pl.ds(2 * step, width)])

    @pl.loop(0, coef // step)
    def _(i):
        chunk(pl.multiple_of(i * step, step), step)

    if coef % step:
        chunk(coef - coef % step, coef % step)
    statistics(scores[...], start, length, stats, all_orients)


def running_body(scores, stats, expon_out, running_out, expon_pad, running_pad, *, rows):
    ori, count = scores.shape
    me = lax.axis_index("orient")
    top = stats[0:1, :]
    if rows:
        top = reorder(top, rows, me)
    carry = jnp.zeros((1, count), jnp.float32)
    sub = lax.broadcasted_iota(jnp.int32, (8, count), 0)
    for o in range(0, ori, 8):
        value = jnp.exp(scores[pl.ds(o, 8), :] - top)
        total = value
        for step in (1, 2, 4):
            total = total + jnp.where(sub >= step, pltpu.roll(total, step, 0), 0.0)
        total = total + carry
        carry = total[7:8, :]
        expon_pad[pl.ds(o, 8), pl.ds(0, count)] = value
        running_pad[pl.ds(o, 8), pl.ds(0, count)] = total
    for o in range(0, ori, LANES):
        width = min(LANES, ori - o)
        for c in range(0, count, LANES):
            high = min(LANES, count - c)
            for pad, out in ((expon_pad, expon_out), (running_pad, running_out)):
                block = pad[pl.ds(o, LANES), pl.ds(c, LANES)].T
                if rows:
                    for b in range(high // rows):
                        place = pl.multiple_of((me ^ b) * rows, rows)
                        out[pl.ds(place, rows), pl.ds(o, width)] = block[b * rows : (b + 1) * rows, :width]
                else:
                    out[pl.ds(c, high), pl.ds(o, width)] = block[:high, :width]


def final_body(near, far, thresholds, start, length, expon, running, *outs, all_orients):
    posterior, cumulative, evidence, mass = outs
    me = lax.axis_index("orient")
    half = near.shape[0] // 4
    tables = [near[pl.ds(4 * b, 4), :] for b in range(half)] + [far[pl.ds(4 * b, 4), :] for b in range(half)]
    top = tables[0][0:1, :]
    for table in tables[1:]:
        top = jnp.maximum(top, table[0:1, :])
    sums = jnp.zeros_like(tables[0])
    shifted = jnp.zeros_like(top)
    for b, table in enumerate(tables):
        scaled = table * jnp.exp(table[0:1, :] - top)
        sums = sums + scaled
        earlier = jnp.where((me ^ b) < me, 1.0, 0.0)
        shifted = shifted + earlier * scaled[1:2, :]
    total = sums[1:2, :]
    evidence[...] = top + jnp.log(total)
    fraction = thresholds[...].astype(jnp.float32) / 1024.0
    wraps = start[...] + length[...] > all_orients
    before = jnp.minimum(sums[2:3, :] / total, fraction)
    until = jnp.minimum(sums[3:4, :] / total, fraction)
    whole = jnp.where(wraps, jnp.minimum(1.0, fraction), 0.0)
    mass[...] = until - before + whole
    scale = column(jnp.exp(tables[0][0:1, :] - top) / total)
    shift = column(shifted / total)
    posterior[...] = expon[...] * scale
    cumulative[...] = running[...] * scale + shift


def call(body, limit, **kwargs):
    params = pltpu.CompilerParams(vmem_limit_bytes=limit)
    return pl.pallas_call(body, compiler_params=params, **kwargs)


def in_vmem(x):
    return pltpu.with_memory_space_constraint(x, pltpu.VMEM)


def in_hbm(x):
    return pltpu.with_memory_space_constraint(x, pltpu.HBM)


def on_device(particles, defocus, inv_noise, references, thresholds, range_start, range_len):
    n = lax.axis_size("orient")
    rows, feat = particles.shape
    coef = inv_noise.shape[0]
    ori = references.shape[0]
    count = n * rows
    all_orients = n * ori
    start = in_vmem(range_start.reshape(1, count))
    length = in_vmem(range_len.reshape(1, count))
    fraction = in_vmem(thresholds.reshape(1, count))
    f32, bf16 = jnp.float32, jnp.bfloat16

    def swap(x, even, odd):
        steps = (even, odd)
        parts = lax.axis_size("dom")
        pairs = [(i * parts + d, (i ^ steps[d % 2]) * parts + d) for i in range(n) for d in range(parts)]
        return lax.ppermute(x, ("orient", "dom"), pairs)

    half = n // 2
    few = n == 8
    packed = call(
        pack_body,
        2**21,
        out_shape=pltpu.VMEM((rows, feat + LANES), bf16),
        in_specs=[HBM, HBM],
        out_specs=VMEM,
        scratch_shapes=[pltpu.VMEM((1, rows), f32), pltpu.SemaphoreType.DMA((2,))],
    )(in_hbm(particles), in_hbm(defocus.reshape(1, rows)))

    local, power = call(
        power_body,
        2**21,
        out_shape=(pltpu.VMEM((ori, feat), bf16), pltpu.VMEM((ori, coef), bf16)),
        in_specs=[HBM],
        out_specs=(VMEM, VMEM),
        scratch_shapes=[pltpu.SemaphoreType.DMA((9,))],
    )(in_hbm(references))
    noise = in_vmem(inv_noise)
    local, power = in_vmem(local), in_vmem(power)
    results = (pltpu.VMEM((ori, count), f32), pltpu.VMEM((4, count), f32))

    if few:
        pieces = {0: packed, half: swap(packed, half, half)}
        for source in (0, half):
            for b in range(half - 1, 0, -1):
                pieces[source ^ b] = swap(pieces[source], b, b)
        stage = pltpu.VMEM((count, 3 * coef), bf16)
        weighted = call(
            weigh_body, 2**22, out_shape=stage, in_specs=[VMEM] * (1 + half), out_specs=VMEM
        )(noise, *[in_vmem(pieces[b]) for b in range(half)])
        scores, stats, _ = call(
            lambda *refs: score_late_body(*refs, row=half * rows, all_orients=all_orients),
            2**23,
            out_shape=results + (stage,),
            in_specs=[VMEM] * (6 + half),
            out_specs=(VMEM,) * 3,
            input_output_aliases={5: 2},
        )(start, length, noise, local, power, in_vmem(weighted), *[in_vmem(pieces[b]) for b in range(half, n)])
    else:
        gathered = lax.all_gather(packed, "orient", axis=0, tiled=True)
        scores, stats = call(
            lambda *refs: score_body(*refs, all_orients=all_orients),
            2**24,
            out_shape=results,
            in_specs=[VMEM] * 6,
            out_specs=(VMEM, VMEM),
            scratch_shapes=[pltpu.VMEM((count, 6 * LANES), bf16)],
        )(start, length, noise, local, power, in_vmem(gathered))

    if few:
        near = jnp.concatenate([stats] + [swap(stats, b, b) for b in range(1, half)], axis=0)
    else:
        near = stats
        b = 1
        while b < half:
            near = jnp.concatenate([near, swap(near, b, b)], axis=0)
            b *= 2
    far = swap(near, half, half)

    pad_ori = -(-ori // LANES) * LANES
    pad_count = -(-count // LANES) * LANES
    expon, running = call(
        lambda *refs: running_body(*refs, rows=rows if few else None),
        2**23,
        out_shape=(pltpu.VMEM((count, ori), f32),) * 2,
        in_specs=[VMEM, VMEM],
        out_specs=(VMEM, VMEM),
        scratch_shapes=[pltpu.VMEM((pad_ori, pad_count), f32)] * 2,
    )(in_vmem(scores), in_vmem(stats))

    posterior, cumulative, evidence, mass = call(
        lambda *refs: final_body(*refs, all_orients=all_orients),
        2**23,
        out_shape=(jax.ShapeDtypeStruct((count, ori), f32),) * 2 + (jax.ShapeDtypeStruct((1, count), f32),) * 2,
        in_specs=[VMEM] * 7,
        out_specs=(VMEM,) * 4,
    )(in_vmem(near), in_vmem(far), fraction, start, length, in_vmem(expon), in_vmem(running))
    return posterior, cumulative, evidence.reshape(count), mass.reshape(count)


def solution(mesh):
    return jax.shard_map(
        on_device,
        mesh=mesh,
        in_specs=(
            P(("dom", "orient"), None),
            P(("dom", "orient")),
            P(),
            P(("dom", "orient"), None),
            P("dom"),
            P("dom"),
            P("dom"),
        ),
        out_specs=(P("dom", "orient"), P("dom", "orient"), P("dom"), P("dom")),
        check_vma=False,
    )
```

profile of v0, /device:TPU:0, one launch (start us, length us, event | category | flops | bytes accessed | tf_op | source)
XLA Modules:
  0.0 37.2 jit_solution(17820979383766956082)
XLA Ops:
  0.6 0.9 %shard_map.103.refs_0_ = bf16[8,8576]{1,0:T(8,128)(2,1)S(1)} custom-call(bf16[8,8448]{1,0:T(8,128)(2,1)} %particles.1, f32[1,8]{1,0:T(1,128)} %bitcast.11), custom_call_target="tpu_custom_call" | custom-call | tf_op jit(solution)/shard_map/pallas_call | solution.py:296
  1.6 4.1 %collective-permute-start.3 = (bf16[8,8576]{1,0:T(8,128)(2,1)S(1)}, bf16[8,8576]{1,0:T(8,128)(2,1)S(1)}, u32[]{:S(2)}, u32[]{:S(2)}) collective-permute-start(bf16[8,8576]{1,0:T(8,128)(2,1)S(1)} %shard_map.103.refs_0_), channel_id=1, source_target_pairs={{0,16},{1,17},{2,18},{3,19},{4,20},{5,21},{6,22},{7,23},{8,24},{9,... | collective-permute-start | bytes 411656 | tf_op jit(solution)/shard_map/ppermute | solution.py:292
  5.7 2.5 %collective-permute-start.2 = (bf16[8,8576]{1,0:T(8,128)(2,1)S(1)}, bf16[8,8576]{1,0:T(8,128)(2,1)S(1)}, u32[]{:S(2)}, u32[]{:S(2)}) collective-permute-start(bf16[8,8576]{1,0:T(8,128)(2,1)S(1)} %shard_map.103.refs_0_), channel_id=1, source_target_pairs={{0,12},{1,13},{2,14},{3,15},{4,8},{5,9},{6,10},{7,11},{8,4},{9,5},... | collective-permute-start | bytes 411656 | tf_op jit(solution)/shard_map/ppermute | solution.py:292
  8.3 0.4 %collective-permute-start.1 = (bf16[8,8576]{1,0:T(8,128)(2,1)S(1)}, bf16[8,8576]{1,0:T(8,128)(2,1)S(1)}, u32[]{:S(2)}, u32[]{:S(2)}) collective-permute-start(bf16[8,8576]{1,0:T(8,128)(2,1)S(1)} %shard_map.103.refs_0_), channel_id=1, source_target_pairs={{0,8},{1,9},{2,10},{3,11},{4,12},{5,13},{6,14},{7,15},{8,0},{9,1},... | collective-permute-start | bytes 411656 | tf_op jit(solution)/shard_map/ppermute | solution.py:292
  8.7 0.5 %collective-permute-start = (bf16[8,8576]{1,0:T(8,128)(2,1)S(1)}, bf16[8,8576]{1,0:T(8,128)(2,1)S(1)}, u32[]{:S(2)}, u32[]{:S(2)}) collective-permute-start(bf16[8,8576]{1,0:T(8,128)(2,1)S(1)} %shard_map.103.refs_0_), channel_id=1, source_target_pairs={{0,4},{1,5},{2,6},{3,7},{4,0},{5,1},{6,2},{7,3},{8,12},{9,13},{10,... | collective-permute-start | bytes 411656 | tf_op jit(solution)/shard_map/ppermute | solution.py:292
  9.2 3.2 %collective-permute-done.3.refs_6_ = bf16[8,8576]{1,0:T(8,128)(2,1)S(1)} collective-permute-done((bf16[8,8576]{1,0:T(8,128)(2,1)S(1)}, bf16[8,8576]{1,0:T(8,128)(2,1)S(1)}, u32[]{:S(2)}, u32[]{:S(2)}) %collective-permute-start.3) | collective-permute-done | bytes 137248 | tf_op jit(solution)/shard_map/ppermute | solution.py:292
  12.4 1.6 %collective-permute-start.6 = (bf16[8,8576]{1,0:T(8,128)(2,1)S(1)}, bf16[8,8576]{1,0:T(8,128)(2,1)S(1)}, u32[]{:S(2)}, u32[]{:S(2)}) collective-permute-start(bf16[8,8576]{1,0:T(8,128)(2,1)S(1)} %collective-permute-done.3.refs_6_), channel_id=1, source_target_pairs={{0,12},{1,13},{2,14},{3,15},{4,8},{5,9},{6,10},{7,11},{8,4},{9,5},... | collective-permute-start | bytes 411656 | tf_op jit(solution)/shard_map/ppermute | solution.py:292
  14.0 1.4 %collective-permute-start.5 = (bf16[8,8576]{1,0:T(8,128)(2,1)S(1)}, bf16[8,8576]{1,0:T(8,128)(2,1)S(1)}, u32[]{:S(2)}, u32[]{:S(2)}) collective-permute-start(bf16[8,8576]{1,0:T(8,128)(2,1)S(1)} %collective-permute-done.3.refs_6_), channel_id=1, source_target_pairs={{0,8},{1,9},{2,10},{3,11},{4,12},{5,13},{6,14},{7,15},{8,0},{9,1},... | collective-permute-start | bytes 411656 | tf_op jit(solution)/shard_map/ppermute | solution.py:292
  15.5 0.6 %collective-permute-start.4 = (bf16[8,8576]{1,0:T(8,128)(2,1)S(1)}, bf16[8,8576]{1,0:T(8,128)(2,1)S(1)}, u32[]{:S(2)}, u32[]{:S(2)}) collective-permute-start(bf16[8,8576]{1,0:T(8,128)(2,1)S(1)} %collective-permute-done.3.refs_6_), channel_id=1, source_target_pairs={{0,4},{1,5},{2,6},{3,7},{4,0},{5,1},{6,2},{7,3},{8,12},{9,13},{10,... | collective-permute-start | bytes 411656 | tf_op jit(solution)/shard_map/ppermute | solution.py:292
  16.1 3.3 %shard_map.102 = (bf16[432,8448]{1,0:T(8,128)(2,1)S(1)}, bf16[432,4224]{1,0:T(8,128)(2,1)S(1)}) custom-call(bf16[432,8448]{1,0:T(8,128)(2,1)} %references.1), custom_call_target="tpu_custom_call" | custom-call | tf_op jit(solution)/shard_map/pallas_call | solution.py:305
  19.4 0.9 %shard_map.104.refs_5_ = bf16[64,12672]{1,0:T(8,128)(2,1)S(1)} custom-call(f32[4224]{0:T(1024)S(1)} %copy-done, bf16[8,8576]{1,0:T(8,128)(2,1)S(1)} %shard_map.103.refs_0_, bf16[8,8576]{1,0:T(8,128)(2,1)S(1)} %collective-permute-done.refs_1_, bf16[8,8576]{1,0:T(8,128)(2,1)S(1)} %collective-permute-done.1.refs_2_, ...), custom_call_target="tpu_custom_call" | custom-call | tf_op jit(solution)/shard_map/pallas_call | solution.py:323
  20.3 0.6 %collective-permute-done.6.refs_9_ = bf16[8,8576]{1,0:T(8,128)(2,1)S(1)} collective-permute-done((bf16[8,8576]{1,0:T(8,128)(2,1)S(1)}, bf16[8,8576]{1,0:T(8,128)(2,1)S(1)}, u32[]{:S(2)}, u32[]{:S(2)}) %collective-permute-start.6) | collective-permute-done | bytes 137248 | tf_op jit(solution)/shard_map/ppermute | solution.py:292
  20.9 1.5 %collective-permute-done.5.refs_8_ = bf16[8,8576]{1,0:T(8,128)(2,1)S(1)} collective-permute-done((bf16[8,8576]{1,0:T(8,128)(2,1)S(1)}, bf16[8,8576]{1,0:T(8,128)(2,1)S(1)}, u32[]{:S(2)}, u32[]{:S(2)}) %collective-permute-start.5) | collective-permute-done | bytes 137248 | tf_op jit(solution)/shard_map/ppermute | solution.py:292
  22.4 3.7 %shard_map.105 = (f32[432,64]{1,0:T(8,128)S(1)}, f32[4,64]{1,0:T(4,128)S(1)}, bf16[64,12672]{1,0:T(8,128)(2,1)S(1)}) custom-call(s32[1,64]{1,0:T(1,128)S(1)} %bitcast.6, s32[1,64]{1,0:T(1,128)S(1)} %bitcast.8, f32[4224]{0:T(1024)S(1)} %copy-done, bf16[432,8448]{1,0:T(8,128)(2,1)S(1)} %get-tuple-element.14.refs_3_, ...), custom_call_target="tpu_custom_call", output_to_operand_aliasing={{2}: (5, {})} | custom-call | tf_op jit(solution)/shard_map/pallas_call | solution.py:326
  26.1 1.5 %collective-permute-start.9 = (f32[4,64]{1,0:T(4,128)S(1)}, f32[4,64]{1,0:T(4,128)S(1)}, u32[]{:S(2)}, u32[]{:S(2)}) collective-permute-start(f32[4,64]{1,0:T(4,128)S(1)} %get-tuple-element.16.refs_1_), channel_id=1, source_target_pairs={{0,12},{1,13},{2,14},{3,15},{4,8},{5,9},{6,10},{7,11},{8,4},{9,5},... | collective-permute-start | bytes 3080 | tf_op jit(solution)/shard_map/ppermute | solution.py:292
  27.6 0.6 %collective-permute-start.8 = (f32[4,64]{1,0:T(4,128)S(1)}, f32[4,64]{1,0:T(4,128)S(1)}, u32[]{:S(2)}, u32[]{:S(2)}) collective-permute-start(f32[4,64]{1,0:T(4,128)S(1)} %get-tuple-element.16.refs_1_), channel_id=1, source_target_pairs={{0,8},{1,9},{2,10},{3,11},{4,12},{5,13},{6,14},{7,15},{8,0},{9,1},... | collective-permute-start | bytes 3080 | tf_op jit(solution)/shard_map/ppermute | solution.py:292
  28.1 1.5 %collective-permute-start.7 = (f32[4,64]{1,0:T(4,128)S(1)}, f32[4,64]{1,0:T(4,128)S(1)}, u32[]{:S(2)}, u32[]{:S(2)}) collective-permute-start(f32[4,64]{1,0:T(4,128)S(1)} %get-tuple-element.16.refs_1_), channel_id=1, source_target_pairs={{0,4},{1,5},{2,6},{3,7},{4,0},{5,1},{6,2},{7,3},{8,12},{9,13},{10,... | collective-permute-start | bytes 3080 | tf_op jit(solution)/shard_map/ppermute | solution.py:292
  29.6 1.0 %collective-permute-done.9 = f32[4,64]{1,0:T(4,128)S(1)} collective-permute-done((f32[4,64]{1,0:T(4,128)S(1)}, f32[4,64]{1,0:T(4,128)S(1)}, u32[]{:S(2)}, u32[]{:S(2)}) %collective-permute-start.9) | collective-permute-done | bytes 1056 | tf_op jit(solution)/shard_map/ppermute | solution.py:292
  30.6 0.6 %collective-permute-done.8 = f32[4,64]{1,0:T(4,128)S(1)} collective-permute-done((f32[4,64]{1,0:T(4,128)S(1)}, f32[4,64]{1,0:T(4,128)S(1)}, u32[]{:S(2)}, u32[]{:S(2)}) %collective-permute-start.8) | collective-permute-done | bytes 1056 | tf_op jit(solution)/shard_map/ppermute | solution.py:292
  31.2 0.6 %collective-permute-done.7 = f32[4,64]{1,0:T(4,128)S(1)} collective-permute-done((f32[4,64]{1,0:T(4,128)S(1)}, f32[4,64]{1,0:T(4,128)S(1)}, u32[]{:S(2)}, u32[]{:S(2)}) %collective-permute-start.7) | collective-permute-done | bytes 1056 | tf_op jit(solution)/shard_map/ppermute | solution.py:292
  31.7 2.5 %collective-permute-start.10 = (f32[16,64]{1,0:T(8,128)S(1)}, f32[16,64]{1,0:T(8,128)S(1)}, u32[]{:S(2)}, u32[]{:S(2)}) collective-permute-start(f32[16,64]{1,0:T(8,128)S(1)} %pad_maximum_fusion.refs_0_), channel_id=1, source_target_pairs={{0,16},{1,17},{2,18},{3,19},{4,20},{5,21},{6,22},{7,23},{8,24},{9,... | collective-permute-start | bytes 12296 | tf_op jit(solution)/shard_map/ppermute | solution.py:292
  34.2 0.5 %shard_map.106 = (f32[64,432]{1,0:T(8,128)S(1)}, f32[64,432]{1,0:T(8,128)S(1)}) custom-call(f32[432,64]{1,0:T(8,128)S(1)} %get-tuple-element.17.refs_0_, f32[4,64]{1,0:T(4,128)S(1)} %get-tuple-element.16.refs_1_), custom_call_target="tpu_custom_call" | custom-call | tf_op jit(solution)/shard_map/pallas_call | solution.py:357
  34.7 1.7 %collective-permute-done.10.refs_1_ = f32[16,64]{1,0:T(8,128)S(1)} collective-permute-done((f32[16,64]{1,0:T(8,128)S(1)}, f32[16,64]{1,0:T(8,128)S(1)}, u32[]{:S(2)}, u32[]{:S(2)}) %collective-permute-start.10) | collective-permute-done | bytes 4128 | tf_op jit(solution)/shard_map/ppermute | solution.py:292
  36.4 0.8 %shard_map.107 = (f32[64,432]{1,0:T(8,128)}, f32[64,432]{1,0:T(8,128)}, f32[1,64]{1,0:T(1,128)}, f32[1,64]{1,0:T(1,128)}) custom-call(f32[16,64]{1,0:T(8,128)S(1)} %pad_maximum_fusion.refs_0_, f32[16,64]{1,0:T(8,128)S(1)} %collective-permute-done.10.refs_1_, s32[1,64]{1,0:T(1,128)S(1)} %bitcast.10, s32[1,64]{1,0:T(1,128)S(1)} %bitcast.7, ...), custom_call_target="tpu_custom_call" | custom-call | tf_op jit(solution)/shard_map/pallas_call | solution.py:366
  (13 shorter events, 0.0 us)
Async XLA Ops:
  1.6 17.8 %copy-start = (f32[4224]{0:T(1024)S(1)}, f32[4224]{0:T(1024)}, u32[]{:S(2)}) copy-start(f32[4224]{0:T(1024)} %refs_2_.1) | copy-start | bytes 50692
  1.6 20.8 %copy-start.1 = (s32[64]{0:T(128)S(1)}, s32[64]{0:T(128)}, u32[]{:S(2)}) copy-start(s32[64]{0:T(128)} %param.12) | copy-start | bytes 772
  1.6 20.8 %copy-start.2 = (s32[64]{0:T(128)S(1)}, s32[64]{0:T(128)}, u32[]{:S(2)}) copy-start(s32[64]{0:T(128)} %param.13) | copy-start | bytes 772
  1.6 10.8 %collective-permute-start.3 = (bf16[8,8576]{1,0:T(8,128)(2,1)S(1)}, bf16[8,8576]{1,0:T(8,128)(2,1)S(1)}, u32[]{:S(2)}, u32[]{:S(2)}) collective-permute-start(bf16[8,8576]{1,0:T(8,128)(2,1)S(1)} %shard_map.103.refs_0_), channel_id=1, source_target_pairs={{0,16},{1,17},{2,18},{3,19},{4,20},{5,21},{6,22},{7,23},{8,24},{9,... | collective-permute-start | bytes 411656 | tf_op jit(solution)/shard_map/ppermute | solution.py:292
  5.7 9.7 %collective-permute-start.2 = (bf16[8,8576]{1,0:T(8,128)(2,1)S(1)}, bf16[8,8576]{1,0:T(8,128)(2,1)S(1)}, u32[]{:S(2)}, u32[]{:S(2)}) collective-permute-start(bf16[8,8576]{1,0:T(8,128)(2,1)S(1)} %shard_map.103.refs_0_), channel_id=1, source_target_pairs={{0,12},{1,13},{2,14},{3,15},{4,8},{5,9},{6,10},{7,11},{8,4},{9,5},... | collective-permute-start | bytes 411656 | tf_op jit(solution)/shard_map/ppermute | solution.py:292
  8.3 11.1 %collective-permute-start.1 = (bf16[8,8576]{1,0:T(8,128)(2,1)S(1)}, bf16[8,8576]{1,0:T(8,128)(2,1)S(1)}, u32[]{:S(2)}, u32[]{:S(2)}) collective-permute-start(bf16[8,8576]{1,0:T(8,128)(2,1)S(1)} %shard_map.103.refs_0_), channel_id=1, source_target_pairs={{0,8},{1,9},{2,10},{3,11},{4,12},{5,13},{6,14},{7,15},{8,0},{9,1},... | collective-permute-start | bytes 411656 | tf_op jit(solution)/shard_map/ppermute | solution.py:292
  8.7 10.7 %collective-permute-start = (bf16[8,8576]{1,0:T(8,128)(2,1)S(1)}, bf16[8,8576]{1,0:T(8,128)(2,1)S(1)}, u32[]{:S(2)}, u32[]{:S(2)}) collective-permute-start(bf16[8,8576]{1,0:T(8,128)(2,1)S(1)} %shard_map.103.refs_0_), channel_id=1, source_target_pairs={{0,4},{1,5},{2,6},{3,7},{4,0},{5,1},{6,2},{7,3},{8,12},{9,13},{10,... | collective-permute-start | bytes 411656 | tf_op jit(solution)/shard_map/ppermute | solution.py:292
  12.4 8.4 %collective-permute-start.6 = (bf16[8,8576]{1,0:T(8,128)(2,1)S(1)}, bf16[8,8576]{1,0:T(8,128)(2,1)S(1)}, u32[]{:S(2)}, u32[]{:S(2)}) collective-permute-start(bf16[8,8576]{1,0:T(8,128)(2,1)S(1)} %collective-permute-done.3.refs_6_), channel_id=1, source_target_pairs={{0,12},{1,13},{2,14},{3,15},{4,8},{5,9},{6,10},{7,11},{8,4},{9,5},... | collective-permute-start | bytes 411656 | tf_op jit(solution)/shard_map/ppermute | solution.py:292
  14.0 8.3 %collective-permute-start.5 = (bf16[8,8576]{1,0:T(8,128)(2,1)S(1)}, bf16[8,8576]{1,0:T(8,128)(2,1)S(1)}, u32[]{:S(2)}, u32[]{:S(2)}) collective-permute-start(bf16[8,8576]{1,0:T(8,128)(2,1)S(1)} %collective-permute-done.3.refs_6_), channel_id=1, source_target_pairs={{0,8},{1,9},{2,10},{3,11},{4,12},{5,13},{6,14},{7,15},{8,0},{9,1},... | collective-permute-start | bytes 411656 | tf_op jit(solution)/shard_map/ppermute | solution.py:292
  15.5 6.9 %collective-permute-start.4 = (bf16[8,8576]{1,0:T(8,128)(2,1)S(1)}, bf16[8,8576]{1,0:T(8,128)(2,1)S(1)}, u32[]{:S(2)}, u32[]{:S(2)}) collective-permute-start(bf16[8,8576]{1,0:T(8,128)(2,1)S(1)} %collective-permute-done.3.refs_6_), channel_id=1, source_target_pairs={{0,4},{1,5},{2,6},{3,7},{4,0},{5,1},{6,2},{7,3},{8,12},{9,13},{10,... | collective-permute-start | bytes 411656 | tf_op jit(solution)/shard_map/ppermute | solution.py:292
  22.4 14.0 %copy-start.3 = (s32[64]{0:T(128)S(1)}, s32[64]{0:T(128)}, u32[]{:S(2)}) copy-start(s32[64]{0:T(128)} %param.11) | copy-start | bytes 772
  26.1 4.5 %collective-permute-start.9 = (f32[4,64]{1,0:T(4,128)S(1)}, f32[4,64]{1,0:T(4,128)S(1)}, u32[]{:S(2)}, u32[]{:S(2)}) collective-permute-start(f32[4,64]{1,0:T(4,128)S(1)} %get-tuple-element.16.refs_1_), channel_id=1, source_target_pairs={{0,12},{1,13},{2,14},{3,15},{4,8},{5,9},{6,10},{7,11},{8,4},{9,5},... | collective-permute-start | bytes 3080 | tf_op jit(solution)/shard_map/ppermute | solution.py:292
  27.6 3.6 %collective-permute-start.8 = (f32[4,64]{1,0:T(4,128)S(1)}, f32[4,64]{1,0:T(4,128)S(1)}, u32[]{:S(2)}, u32[]{:S(2)}) collective-permute-start(f32[4,64]{1,0:T(4,128)S(1)} %get-tuple-element.16.refs_1_), channel_id=1, source_target_pairs={{0,8},{1,9},{2,10},{3,11},{4,12},{5,13},{6,14},{7,15},{8,0},{9,1},... | collective-permute-start | bytes 3080 | tf_op jit(solution)/shard_map/ppermute | solution.py:292
  28.1 3.6 %collective-permute-start.7 = (f32[4,64]{1,0:T(4,128)S(1)}, f32[4,64]{1,0:T(4,128)S(1)}, u32[]{:S(2)}, u32[]{:S(2)}) collective-permute-start(f32[4,64]{1,0:T(4,128)S(1)} %get-tuple-element.16.refs_1_), channel_id=1, source_target_pairs={{0,4},{1,5},{2,6},{3,7},{4,0},{5,1},{6,2},{7,3},{8,12},{9,13},{10,... | collective-permute-start | bytes 3080 | tf_op jit(solution)/shard_map/ppermute | solution.py:292
  31.7 4.6 %collective-permute-start.10 = (f32[16,64]{1,0:T(8,128)S(1)}, f32[16,64]{1,0:T(8,128)S(1)}, u32[]{:S(2)}, u32[]{:S(2)}) collective-permute-start(f32[16,64]{1,0:T(8,128)S(1)} %pad_maximum_fusion.refs_0_), channel_id=1, source_target_pairs={{0,16},{1,17},{2,18},{3,19},{4,20},{5,21},{6,22},{7,23},{8,24},{9,... | collective-permute-start | bytes 12296 | tf_op jit(solution)/shard_map/ppermute | solution.py:292
where the time goes:
time: 37.3 us; the launch traced here: 37.2 us
  starting transfers between devices  17.2 us (46%)
  Pallas kernels  10.2 us (27%)
  waiting for transfers between devices  9.05 us (24%)
  between operations  0.72 us (2%)
    ppermute x11, starting transfers between devices, swap(): return lax.ppermute(x, ('orient', 'dom'), pairs)  17.2 us
    ppermute x11, waiting for transfers between devices, swap(): return lax.ppermute(x, ('orient', 'dom'), pairs)  9.05 us
    pallas_call x1, Pallas kernels, on_device(): call(lambda *refs: score_late_body(*refs, row=half * rows, all_orients=al...  3.7 us
    pallas_call x1, Pallas kernels, on_device(): call(power_body, 2 ** 21, out_shape=(pltpu.VMEM((ori, feat), bf16), pltpu...  3.32 us
    pallas_call x1, Pallas kernels, on_device(): call(pack_body, 2 ** 21, out_shape=pltpu.VMEM((rows, feat + LANES), bf16)...  0.94 us
    pallas_call x1, Pallas kernels, on_device(): call(weigh_body, 2 ** 22, out_shape=stage, in_specs=[VMEM] * (1 + half),...  0.88 us
    pallas_call x1, Pallas kernels, on_device(): call(lambda *refs: final_body(*refs, all_orients=all_orients), 2 ** 23, o...  0.83 us
  transfers between devices with their start and end apart: 11, of which 7 were waited for; matrix products, arithmetic and copies ran while one was open for 0% of the time, Pallas kernels for 13%

commit v1 on v0

--- a/solution.py
+++ b/solution.py
@@ -36,10 +36,13 @@
 
 def pack_body(particles, defocus, out, row, sems):
     feat = particles.shape[1]
-    copy = pltpu.make_async_copy(particles, out.at[:, pl.ds(0, feat)], sems.at[0])
-    fetch = pltpu.make_async_copy(defocus, row, sems.at[1])
+    width = -(-feat // (LANES * (sems.shape[0] - 1))) * LANES
+    spans = [pl.ds(k, min(width, feat - k)) for k in range(0, feat, width)]
+    copies = [pltpu.make_async_copy(particles.at[:, span], out.at[:, span], sems.at[i + 1]) for i, span in enumerate(spans)]
+    fetch = pltpu.make_async_copy(defocus, row, sems.at[0])
     fetch.start()
-    copy.start()
+    for copy in copies:
+        copy.start()
     fetch.wait()
     value = column(row[...])
     high = value.astype(jnp.bfloat16).astype(jnp.float32)
@@ -48,7 +51,8 @@
     lane = lax.broadcasted_iota(jnp.int32, (value.shape[0], LANES), 1)
     parts = jnp.where(lane == 0, high, jnp.where(lane == 1, mid, jnp.where(lane == 2, low, 0.0)))
     out[:, pl.ds(feat, LANES)] = parts.astype(jnp.bfloat16)
-    copy.wait()
+    for copy in copies:
+        copy.wait()
 
 
 def focus_of(piece, cut):
@@ -299,7 +303,7 @@
         out_shape=pltpu.VMEM((rows, feat + LANES), bf16),
         in_specs=[HBM, HBM],
         out_specs=VMEM,
-        scratch_shapes=[pltpu.VMEM((1, rows), f32), pltpu.SemaphoreType.DMA((2,))],
+        scratch_shapes=[pltpu.VMEM((1, rows), f32), pltpu.SemaphoreType.DMA((7,))],
     )(in_hbm(particles), in_hbm(defocus.reshape(1, rows)))
 
     local, power = call(

time: 37.3 us -> 37.3 us (level)
  no operation moved by 1% of the time
where the time goes in v1:
time: 37.3 us; the launch traced here: 37.1 us
  starting transfers between devices  17.2 us (46%)
  Pallas kernels  10.1 us (27%)
  waiting for transfers between devices  9.04 us (24%)
  between operations  0.72 us (2%)
    ppermute x11, starting transfers between devices, swap(): return lax.ppermute(x, ('orient', 'dom'), pairs)  17.2 us
    ppermute x11, waiting for transfers between devices, swap(): return lax.ppermute(x, ('orient', 'dom'), pairs)  9.04 us
    pallas_call x1, Pallas kernels, on_device(): call(lambda *refs: score_late_body(*refs, row=half * rows, all_orients=al...  3.7 us
    pallas_call x1, Pallas kernels, on_device(): call(power_body, 2 ** 21, out_shape=(pltpu.VMEM((ori, feat), bf16), pltpu...  3.32 us
    pallas_call x1, Pallas kernels, on_device(): call(pack_body, 2 ** 21, out_shape=pltpu.VMEM((rows, feat + LANES), bf16)...  0.9 us
    pallas_call x1, Pallas kernels, on_device(): call(weigh_body, 2 ** 22, out_shape=stage, in_specs=[VMEM] * (1 + half),...  0.88 us
    pallas_call x1, Pallas kernels, on_device(): call(lambda *refs: final_body(*refs, all_orients=all_orients), 2 ** 23, o...  0.83 us
  transfers between devices with their start and end apart: 11, of which 7 were waited for; matrix products, arithmetic and copies ran while one was open for 0% of the time, Pallas kernels for 13%

profile of v1, /device:TPU:0, one launch (start us, length us, event | category | flops | bytes accessed | tf_op | source)
XLA Modules:
  0.0 37.1 jit_solution(6195774707273804665)
XLA Ops:
  0.6 0.9 %shard_map.103.refs_0_ = bf16[8,8576]{1,0:T(8,128)(2,1)S(1)} custom-call(bf16[8,8448]{1,0:T(8,128)(2,1)} %particles.1, f32[1,8]{1,0:T(1,128)} %bitcast.11), custom_call_target="tpu_custom_call" | custom-call | tf_op jit(solution)/shard_map/pallas_call | solution.py:300
  1.6 4.1 %collective-permute-start.3 = (bf16[8,8576]{1,0:T(8,128)(2,1)S(1)}, bf16[8,8576]{1,0:T(8,128)(2,1)S(1)}, u32[]{:S(2)}, u32[]{:S(2)}) collective-permute-start(bf16[8,8576]{1,0:T(8,128)(2,1)S(1)} %shard_map.103.refs_0_), channel_id=1, source_target_pairs={{0,16},{1,17},{2,18},{3,19},{4,20},{5,21},{6,22},{7,23},{8,24},{9,... | collective-permute-start | bytes 411656 | tf_op jit(solution)/shard_map/ppermute | solution.py:296
  5.7 2.5 %collective-permute-start.2 = (bf16[8,8576]{1,0:T(8,128)(2,1)S(1)}, bf16[8,8576]{1,0:T(8,128)(2,1)S(1)}, u32[]{:S(2)}, u32[]{:S(2)}) collective-permute-start(bf16[8,8576]{1,0:T(8,128)(2,1)S(1)} %shard_map.103.refs_0_), channel_id=1, source_target_pairs={{0,12},{1,13},{2,14},{3,15},{4,8},{5,9},{6,10},{7,11},{8,4},{9,5},... | collective-permute-start | bytes 411656 | tf_op jit(solution)/shard_map/ppermute | solution.py:296
  8.2 0.4 %collective-permute-start.1 = (bf16[8,8576]{1,0:T(8,128)(2,1)S(1)}, bf16[8,8576]{1,0:T(8,128)(2,1)S(1)}, u32[]{:S(2)}, u32[]{:S(2)}) collective-permute-start(bf16[8,8576]{1,0:T(8,128)(2,1)S(1)} %shard_map.103.refs_0_), channel_id=1, source_target_pairs={{0,8},{1,9},{2,10},{3,11},{4,12},{5,13},{6,14},{7,15},{8,0},{9,1},... | collective-permute-start | bytes 411656 | tf_op jit(solution)/shard_map/ppermute | solution.py:296
  8.7 0.5 %collective-permute-start = (bf16[8,8576]{1,0:T(8,128)(2,1)S(1)}, bf16[8,8576]{1,0:T(8,128)(2,1)S(1)}, u32[]{:S(2)}, u32[]{:S(2)}) collective-permute-start(bf16[8,8576]{1,0:T(8,128)(2,1)S(1)} %shard_map.103.refs_0_), channel_id=1, source_target_pairs={{0,4},{1,5},{2,6},{3,7},{4,0},{5,1},{6,2},{7,3},{8,12},{9,13},{10,... | collective-permute-start | bytes 411656 | tf_op jit(solution)/shard_map/ppermute | solution.py:296
  9.2 3.2 %collective-permute-done.3.refs_6_ = bf16[8,8576]{1,0:T(8,128)(2,1)S(1)} collective-permute-done((bf16[8,8576]{1,0:T(8,128)(2,1)S(1)}, bf16[8,8576]{1,0:T(8,128)(2,1)S(1)}, u32[]{:S(2)}, u32[]{:S(2)}) %collective-permute-start.3) | collective-permute-done | bytes 137248 | tf_op jit(solution)/shard_map/ppermute | solution.py:296
  12.4 1.6 %collective-permute-start.6 = (bf16[8,8576]{1,0:T(8,128)(2,1)S(1)}, bf16[8,8576]{1,0:T(8,128)(2,1)S(1)}, u32[]{:S(2)}, u32[]{:S(2)}) collective-permute-start(bf16[8,8576]{1,0:T(8,128)(2,1)S(1)} %collective-permute-done.3.refs_6_), channel_id=1, source_target_pairs={{0,12},{1,13},{2,14},{3,15},{4,8},{5,9},{6,10},{7,11},{8,4},{9,5},... | collective-permute-start | bytes 411656 | tf_op jit(solution)/shard_map/ppermute | solution.py:296
  14.0 1.4 %collective-permute-start.5 = (bf16[8,8576]{1,0:T(8,128)(2,1)S(1)}, bf16[8,8576]{1,0:T(8,128)(2,1)S(1)}, u32[]{:S(2)}, u32[]{:S(2)}) collective-permute-start(bf16[8,8576]{1,0:T(8,128)(2,1)S(1)} %collective-permute-done.3.refs_6_), channel_id=1, source_target_pairs={{0,8},{1,9},{2,10},{3,11},{4,12},{5,13},{6,14},{7,15},{8,0},{9,1},... | collective-permute-start | bytes 411656 | tf_op jit(solution)/shard_map/ppermute | solution.py:296
  15.4 0.6 %collective-permute-start.4 = (bf16[8,8576]{1,0:T(8,128)(2,1)S(1)}, bf16[8,8576]{1,0:T(8,128)(2,1)S(1)}, u32[]{:S(2)}, u32[]{:S(2)}) collective-permute-start(bf16[8,8576]{1,0:T(8,128)(2,1)S(1)} %collective-permute-done.3.refs_6_), channel_id=1, source_target_pairs={{0,4},{1,5},{2,6},{3,7},{4,0},{5,1},{6,2},{7,3},{8,12},{9,13},{10,... | collective-permute-start | bytes 411656 | tf_op jit(solution)/shard_map/ppermute | solution.py:296
  16.0 3.3 %shard_map.102 = (bf16[432,8448]{1,0:T(8,128)(2,1)S(1)}, bf16[432,4224]{1,0:T(8,128)(2,1)S(1)}) custom-call(bf16[432,8448]{1,0:T(8,128)(2,1)} %references.1), custom_call_target="tpu_custom_call" | custom-call | tf_op jit(solution)/shard_map/pallas_call | solution.py:309
  19.4 0.9 %shard_map.104.refs_5_ = bf16[64,12672]{1,0:T(8,128)(2,1)S(1)} custom-call(f32[4224]{0:T(1024)S(1)} %copy-done, bf16[8,8576]{1,0:T(8,128)(2,1)S(1)} %shard_map.103.refs_0_, bf16[8,8576]{1,0:T(8,128)(2,1)S(1)} %collective-permute-done.refs_1_, bf16[8,8576]{1,0:T(8,128)(2,1)S(1)} %collective-permute-done.1.refs_2_, ...), custom_call_target="tpu_custom_call" | custom-call | tf_op jit(solution)/shard_map/pallas_call | solution.py:327
  20.3 0.6 %collective-permute-done.6.refs_9_ = bf16[8,8576]{1,0:T(8,128)(2,1)S(1)} collective-permute-done((bf16[8,8576]{1,0:T(8,128)(2,1)S(1)}, bf16[8,8576]{1,0:T(8,128)(2,1)S(1)}, u32[]{:S(2)}, u32[]{:S(2)}) %collective-permute-start.6) | collective-permute-done | bytes 137248 | tf_op jit(solution)/shard_map/ppermute | solution.py:296
  20.8 1.5 %collective-permute-done.5.refs_8_ = bf16[8,8576]{1,0:T(8,128)(2,1)S(1)} collective-permute-done((bf16[8,8576]{1,0:T(8,128)(2,1)S(1)}, bf16[8,8576]{1,0:T(8,128)(2,1)S(1)}, u32[]{:S(2)}, u32[]{:S(2)}) %collective-permute-start.5) | collective-permute-done | bytes 137248 | tf_op jit(solution)/shard_map/ppermute | solution.py:296
  22.4 3.7 %shard_map.105 = (f32[432,64]{1,0:T(8,128)S(1)}, f32[4,64]{1,0:T(4,128)S(1)}, bf16[64,12672]{1,0:T(8,128)(2,1)S(1)}) custom-call(s32[1,64]{1,0:T(1,128)S(1)} %bitcast.6, s32[1,64]{1,0:T(1,128)S(1)} %bitcast.8, f32[4224]{0:T(1024)S(1)} %copy-done, bf16[432,8448]{1,0:T(8,128)(2,1)S(1)} %get-tuple-element.14.refs_3_, ...), custom_call_target="tpu_custom_call", output_to_operand_aliasing={{2}: (5, {})} | custom-call | tf_op jit(solution)/shard_map/pallas_call | solution.py:330
  26.1 1.5 %collective-permute-start.9 = (f32[4,64]{1,0:T(4,128)S(1)}, f32[4,64]{1,0:T(4,128)S(1)}, u32[]{:S(2)}, u32[]{:S(2)}) collective-permute-start(f32[4,64]{1,0:T(4,128)S(1)} %get-tuple-element.16.refs_1_), channel_id=1, source_target_pairs={{0,12},{1,13},{2,14},{3,15},{4,8},{5,9},{6,10},{7,11},{8,4},{9,5},... | collective-permute-start | bytes 3080 | tf_op jit(solution)/shard_map/ppermute | solution.py:296
  27.5 0.6 %collective-permute-start.8 = (f32[4,64]{1,0:T(4,128)S(1)}, f32[4,64]{1,0:T(4,128)S(1)}, u32[]{:S(2)}, u32[]{:S(2)}) collective-permute-start(f32[4,64]{1,0:T(4,128)S(1)} %get-tuple-element.16.refs_1_), channel_id=1, source_target_pairs={{0,8},{1,9},{2,10},{3,11},{4,12},{5,13},{6,14},{7,15},{8,0},{9,1},... | collective-permute-start | bytes 3080 | tf_op jit(solution)/shard_map/ppermute | solution.py:296
  28.1 1.5 %collective-permute-start.7 = (f32[4,64]{1,0:T(4,128)S(1)}, f32[4,64]{1,0:T(4,128)S(1)}, u32[]{:S(2)}, u32[]{:S(2)}) collective-permute-start(f32[4,64]{1,0:T(4,128)S(1)} %get-tuple-element.16.refs_1_), channel_id=1, source_target_pairs={{0,4},{1,5},{2,6},{3,7},{4,0},{5,1},{6,2},{7,3},{8,12},{9,13},{10,... | collective-permute-start | bytes 3080 | tf_op jit(solution)/shard_map/ppermute | solution.py:296
  29.6 1.0 %collective-permute-done.9 = f32[4,64]{1,0:T(4,128)S(1)} collective-permute-done((f32[4,64]{1,0:T(4,128)S(1)}, f32[4,64]{1,0:T(4,128)S(1)}, u32[]{:S(2)}, u32[]{:S(2)}) %collective-permute-start.9) | collective-permute-done | bytes 1056 | tf_op jit(solution)/shard_map/ppermute | solution.py:296
  30.6 0.6 %collective-permute-done.8 = f32[4,64]{1,0:T(4,128)S(1)} collective-permute-done((f32[4,64]{1,0:T(4,128)S(1)}, f32[4,64]{1,0:T(4,128)S(1)}, u32[]{:S(2)}, u32[]{:S(2)}) %collective-permute-start.8) | collective-permute-done | bytes 1056 | tf_op jit(solution)/shard_map/ppermute | solution.py:296
  31.1 0.6 %collective-permute-done.7 = f32[4,64]{1,0:T(4,128)S(1)} collective-permute-done((f32[4,64]{1,0:T(4,128)S(1)}, f32[4,64]{1,0:T(4,128)S(1)}, u32[]{:S(2)}, u32[]{:S(2)}) %collective-permute-start.7) | collective-permute-done | bytes 1056 | tf_op jit(solution)/shard_map/ppermute | solution.py:296
  31.7 2.5 %collective-permute-start.10 = (f32[16,64]{1,0:T(8,128)S(1)}, f32[16,64]{1,0:T(8,128)S(1)}, u32[]{:S(2)}, u32[]{:S(2)}) collective-permute-start(f32[16,64]{1,0:T(8,128)S(1)} %pad_maximum_fusion.refs_0_), channel_id=1, source_target_pairs={{0,16},{1,17},{2,18},{3,19},{4,20},{5,21},{6,22},{7,23},{8,24},{9,... | collective-permute-start | bytes 12296 | tf_op jit(solution)/shard_map/ppermute | solution.py:296
  34.2 0.5 %shard_map.106 = (f32[64,432]{1,0:T(8,128)S(1)}, f32[64,432]{1,0:T(8,128)S(1)}) custom-call(f32[432,64]{1,0:T(8,128)S(1)} %get-tuple-element.17.refs_0_, f32[4,64]{1,0:T(4,128)S(1)} %get-tuple-element.16.refs_1_), custom_call_target="tpu_custom_call" | custom-call | tf_op jit(solution)/shard_map/pallas_call | solution.py:361
  34.7 1.6 %collective-permute-done.10.refs_1_ = f32[16,64]{1,0:T(8,128)S(1)} collective-permute-done((f32[16,64]{1,0:T(8,128)S(1)}, f32[16,64]{1,0:T(8,128)S(1)}, u32[]{:S(2)}, u32[]{:S(2)}) %collective-permute-start.10) | collective-permute-done | bytes 4128 | tf_op jit(solution)/shard_map/ppermute | solution.py:296
  36.3 0.8 %shard_map.107 = (f32[64,432]{1,0:T(8,128)}, f32[64,432]{1,0:T(8,128)}, f32[1,64]{1,0:T(1,128)}, f32[1,64]{1,0:T(1,128)}) custom-call(f32[16,64]{1,0:T(8,128)S(1)} %pad_maximum_fusion.refs_0_, f32[16,64]{1,0:T(8,128)S(1)} %collective-permute-done.10.refs_1_, s32[1,64]{1,0:T(1,128)S(1)} %bitcast.10, s32[1,64]{1,0:T(1,128)S(1)} %bitcast.7, ...), custom_call_target="tpu_custom_call" | custom-call | tf_op jit(solution)/shard_map/pallas_call | solution.py:370
  (13 shorter events, 0.0 us)
Async XLA Ops:
  1.5 17.8 %copy-start = (f32[4224]{0:T(1024)S(1)}, f32[4224]{0:T(1024)}, u32[]{:S(2)}) copy-start(f32[4224]{0:T(1024)} %refs_2_.1) | copy-start | bytes 50692
  1.5 20.8 %copy-start.1 = (s32[64]{0:T(128)S(1)}, s32[64]{0:T(128)}, u32[]{:S(2)}) copy-start(s32[64]{0:T(128)} %param.12) | copy-start | bytes 772
  1.6 20.8 %copy-start.2 = (s32[64]{0:T(128)S(1)}, s32[64]{0:T(128)}, u32[]{:S(2)}) copy-start(s32[64]{0:T(128)} %param.13) | copy-start | bytes 772
  1.6 10.8 %collective-permute-start.3 = (bf16[8,8576]{1,0:T(8,128)(2,1)S(1)}, bf16[8,8576]{1,0:T(8,128)(2,1)S(1)}, u32[]{:S(2)}, u32[]{:S(2)}) collective-permute-start(bf16[8,8576]{1,0:T(8,128)(2,1)S(1)} %shard_map.103.refs_0_), channel_id=1, source_target_pairs={{0,16},{1,17},{2,18},{3,19},{4,20},{5,21},{6,22},{7,23},{8,24},{9,... | collective-permute-start | bytes 411656 | tf_op jit(solution)/shard_map/ppermute | solution.py:296
  5.7 9.7 %collective-permute-start.2 = (bf16[8,8576]{1,0:T(8,128)(2,1)S(1)}, bf16[8,8576]{1,0:T(8,128)(2,1)S(1)}, u32[]{:S(2)}, u32[]{:S(2)}) collective-permute-start(bf16[8,8576]{1,0:T(8,128)(2,1)S(1)} %shard_map.103.refs_0_), channel_id=1, source_target_pairs={{0,12},{1,13},{2,14},{3,15},{4,8},{5,9},{6,10},{7,11},{8,4},{9,5},... | collective-permute-start | bytes 411656 | tf_op jit(solution)/shard_map/ppermute | solution.py:296
  8.2 11.1 %collective-permute-start.1 = (bf16[8,8576]{1,0:T(8,128)(2,1)S(1)}, bf16[8,8576]{1,0:T(8,128)(2,1)S(1)}, u32[]{:S(2)}, u32[]{:S(2)}) collective-permute-start(bf16[8,8576]{1,0:T(8,128)(2,1)S(1)} %shard_map.103.refs_0_), channel_id=1, source_target_pairs={{0,8},{1,9},{2,10},{3,11},{4,12},{5,13},{6,14},{7,15},{8,0},{9,1},... | collective-permute-start | bytes 411656 | tf_op jit(solution)/shard_map/ppermute | solution.py:296
  8.7 10.7 %collective-permute-start = (bf16[8,8576]{1,0:T(8,128)(2,1)S(1)}, bf16[8,8576]{1,0:T(8,128)(2,1)S(1)}, u32[]{:S(2)}, u32[]{:S(2)}) collective-permute-start(bf16[8,8576]{1,0:T(8,128)(2,1)S(1)} %shard_map.103.refs_0_), channel_id=1, source_target_pairs={{0,4},{1,5},{2,6},{3,7},{4,0},{5,1},{6,2},{7,3},{8,12},{9,13},{10,... | collective-permute-start | bytes 411656 | tf_op jit(solution)/shard_map/ppermute | solution.py:296
  12.4 8.4 %collective-permute-start.6 = (bf16[8,8576]{1,0:T(8,128)(2,1)S(1)}, bf16[8,8576]{1,0:T(8,128)(2,1)S(1)}, u32[]{:S(2)}, u32[]{:S(2)}) collective-permute-start(bf16[8,8576]{1,0:T(8,128)(2,1)S(1)} %collective-permute-done.3.refs_6_), channel_id=1, source_target_pairs={{0,12},{1,13},{2,14},{3,15},{4,8},{5,9},{6,10},{7,11},{8,4},{9,5},... | collective-permute-start | bytes 411656 | tf_op jit(solution)/shard_map/ppermute | solution.py:296
  14.0 8.3 %collective-permute-start.5 = (bf16[8,8576]{1,0:T(8,128)(2,1)S(1)}, bf16[8,8576]{1,0:T(8,128)(2,1)S(1)}, u32[]{:S(2)}, u32[]{:S(2)}) collective-permute-start(bf16[8,8576]{1,0:T(8,128)(2,1)S(1)} %collective-permute-done.3.refs_6_), channel_id=1, source_target_pairs={{0,8},{1,9},{2,10},{3,11},{4,12},{5,13},{6,14},{7,15},{8,0},{9,1},... | collective-permute-start | bytes 411656 | tf_op jit(solution)/shard_map/ppermute | solution.py:296
  15.4 6.9 %collective-permute-start.4 = (bf16[8,8576]{1,0:T(8,128)(2,1)S(1)}, bf16[8,8576]{1,0:T(8,128)(2,1)S(1)}, u32[]{:S(2)}, u32[]{:S(2)}) collective-permute-start(bf16[8,8576]{1,0:T(8,128)(2,1)S(1)} %collective-permute-done.3.refs_6_), channel_id=1, source_target_pairs={{0,4},{1,5},{2,6},{3,7},{4,0},{5,1},{6,2},{7,3},{8,12},{9,13},{10,... | collective-permute-start | bytes 411656 | tf_op jit(solution)/shard_map/ppermute | solution.py:296
  22.4 14.0 %copy-start.3 = (s32[64]{0:T(128)S(1)}, s32[64]{0:T(128)}, u32[]{:S(2)}) copy-start(s32[64]{0:T(128)} %param.11) | copy-start | bytes 772
  26.1 4.5 %collective-permute-start.9 = (f32[4,64]{1,0:T(4,128)S(1)}, f32[4,64]{1,0:T(4,128)S(1)}, u32[]{:S(2)}, u32[]{:S(2)}) collective-permute-start(f32[4,64]{1,0:T(4,128)S(1)} %get-tuple-element.16.refs_1_), channel_id=1, source_target_pairs={{0,12},{1,13},{2,14},{3,15},{4,8},{5,9},{6,10},{7,11},{8,4},{9,5},... | collective-permute-start | bytes 3080 | tf_op jit(solution)/shard_map/ppermute | solution.py:296
  27.5 3.6 %collective-permute-start.8 = (f32[4,64]{1,0:T(4,128)S(1)}, f32[4,64]{1,0:T(4,128)S(1)}, u32[]{:S(2)}, u32[]{:S(2)}) collective-permute-start(f32[4,64]{1,0:T(4,128)S(1)} %get-tuple-element.16.refs_1_), channel_id=1, source_target_pairs={{0,8},{1,9},{2,10},{3,11},{4,12},{5,13},{6,14},{7,15},{8,0},{9,1},... | collective-permute-start | bytes 3080 | tf_op jit(solution)/shard_map/ppermute | solution.py:296
  28.1 3.6 %collective-permute-start.7 = (f32[4,64]{1,0:T(4,128)S(1)}, f32[4,64]{1,0:T(4,128)S(1)}, u32[]{:S(2)}, u32[]{:S(2)}) collective-permute-start(f32[4,64]{1,0:T(4,128)S(1)} %get-tuple-element.16.refs_1_), channel_id=1, source_target_pairs={{0,4},{1,5},{2,6},{3,7},{4,0},{5,1},{6,2},{7,3},{8,12},{9,13},{10,... | collective-permute-start | bytes 3080 | tf_op jit(solution)/shard_map/ppermute | solution.py:296
  31.7 4.6 %collective-permute-start.10 = (f32[16,64]{1,0:T(8,128)S(1)}, f32[16,64]{1,0:T(8,128)S(1)}, u32[]{:S(2)}, u32[]{:S(2)}) collective-permute-start(f32[16,64]{1,0:T(8,128)S(1)} %pad_maximum_fusion.refs_0_), channel_id=1, source_target_pairs={{0,16},{1,17},{2,18},{3,19},{4,20},{5,21},{6,22},{7,23},{8,24},{9,... | collective-permute-start | bytes 12296 | tf_op jit(solution)/shard_map/ppermute | solution.py:296
